TPU v7x, 32 devices: a whole 2x2x4 slice. The times are simulated.
32 devices in a mesh: row: 8 (over z, core), col: 4 (over y, x).
Axes of the slice: x: 2, y: 2, z: 4, core: 2. Of those that a mesh axis runs over, the one named last changes fastest.
Arguments:
- inverse_tiles: bfloat16 [12288, 12288], P('row', 'col'), may hold values from -6 to 6
- factor: bfloat16 [12288, 2048], P('row', 'col'), may hold values from -0.0546875 to 0.0546875
- block_mask: int32 [96, 16], replicated, may hold values 0 or 1
- diag_inverse: float32 [16, 128, 128], replicated, may hold values from -6 to 6
Outputs:
- off_block: bfloat16 [2048, 12288], P('col', 'row')
- diag_block: float32 [16, 128, 128], P('col')
All inputs are finite; a program needn't handle non-finite values.
Results may differ from a plain program's by a relative error of at most 0.012.
Values may be sent and summed in bfloat16 or wider, within the bound.
No kernel may reach another device: no remote copies, remote signals or barrier semaphores. Data moves between devices by JAX's collectives and lax.ppermute only.
A program may use at most 128 MiB of HBM per device.

v0:
```python
import jax
import jax.numpy as jnp
from jax import lax
from jax.sharding import PartitionSpec as P


def from_root(value, axis, source):
    kept = jnp.where(lax.axis_index(axis) == source, value, 0).astype(value.dtype)
    return lax.psum(kept, axis)


def per_device(inverse_tiles, factor, block_mask, diag_inverse):
    rows_here, cols_here = factor.shape
    block_width = diag_inverse.shape[1]
    sup_here = cols_here // block_width
    blocks_here = rows_here // block_width
    row_index = lax.axis_index("row")
    col_index = lax.axis_index("col")
    mask_here = lax.dynamic_slice(
        block_mask, (row_index * blocks_here, col_index * sup_here), (blocks_here, sup_here)
    )
    keep_mask = jnp.repeat(jnp.repeat(mask_here, block_width, 0), block_width, 1).astype(
        jnp.bfloat16
    )
    masked = factor * keep_mask
    full_rows = lax.all_gather(masked, "col", axis=1, tiled=True)
    row_ratio = lax.axis_size("row") // lax.axis_size("col")
    row_pieces = []
    for offset in range(row_ratio):
        row_pieces.append(from_root(full_rows, "row", row_ratio * col_index + offset))
    summed = jnp.zeros((full_rows.shape[1], rows_here), jnp.float32)
    for offset in range(row_ratio):
        columns = row_pieces[offset]
        inverse_part = inverse_tiles[:, offset * rows_here : (offset + 1) * rows_here]
        summed = summed + lax.dot_general(
            columns, inverse_part, (((0,), (1,)), ((), ())), preferred_element_type=jnp.float32
        )
    reduced = lax.psum_scatter(summed, "col", scatter_dimension=0, tiled=True)
    left_factor = masked.astype(jnp.float32).reshape(rows_here, sup_here, block_width)
    right_product = reduced.reshape(sup_here, block_width, rows_here)
    partial_diag = jnp.einsum(
        "jbr,rja->jab", right_product, left_factor, precision=lax.Precision.HIGHEST
    )
    summed_diag = lax.psum(partial_diag.astype(jnp.bfloat16), "row").astype(jnp.float32)
    own_diag = lax.dynamic_slice_in_dim(diag_inverse, col_index * sup_here, sup_here, 0)
    return ((-reduced).astype(jnp.bfloat16), own_diag + summed_diag)


def solution(mesh):
    return jax.shard_map(
        per_device,
        mesh=mesh,
        in_specs=(P("row", "col"), P("row", "col"), P(), P()),
        out_specs=(P("col", "row"), P("col", None, None)),
        check_vma=False,
    )
```

profile of v0, /device:TPU:0, one launch (start us, length us, event | category | flops | bytes accessed | tf_op | source)
XLA Modules:
  0.0 571.0 jit_solution(12963636259537801392)
XLA Ops:
  7.2 0.0 all-gather.2.cloned.1.call-start
  7.2 0.8 dynamic-slice_convert_fusion
  8.0 0.1 copy.6
  8.1 0.1 broadcast_in_dim.11
  8.2 1.9 broadcast_in_dim.12
  10.1 2.8 bitcast_multiply_fusion
  12.9 0.0 all-gather.2.cloned.1.call-update
  12.9 0.0 all-reduce.6.cloned.1.call-start
  12.9 72.7 %all-gather.2.cloned.1.call-done = bf16[1536,2048]{1,0:T(8,128)(2,1)} async-done(((bf16[1536,512]{1,0:T(8,128)(2,1)}), bf16[1536,2048]{1,0:T(8,128)(2,1)}) %all-gather.2.cloned.1.call-update) | async-done | bytes 6291472 | tf_op jit(solution)/shard_map/all_gather | solution.py:26
  85.7 8.1 %broadcast_select_fusion = (bf16[1536,2048]{1,0:T(8,128)(2,1)}, bf16[1536,2048]{1,0:T(8,128)(2,1)}) fusion(bf16[1536,2048]{1,0:T(8,128)(2,1)} %all-gather.2.cloned.1.call-done, pred[]{:T(512)S(6)} %eq.7, pred[]{:T(512)S(6)} %eq.6), kind=kLoop, calls=%fused_computation.1 | loop fusion | flops 6291456 | bytes 18874370 | tf_op jit(solution)/shard_map/jit(_where)/select_n | solution.py:8
  93.8 0.0 slice-start
  93.8 0.0 all-reduce.6.cloned.1.call-update
  93.8 0.0 reduce-scatter.2.cloned.1.call-start
  93.9 254.7 %all-reduce.6.cloned.1.call-done = (bf16[1536,2048]{1,0:T(8,128)(2,1)}, bf16[1536,2048]{1,0:T(8,128)(2,1)}) async-done(((bf16[1536,2048]{1,0:T(8,128)(2,1)}, bf16[1536,2048]{1,0:T(8,128)(2,1)}), (bf16[1536,2048]{1,0:T(8,128)(2,1)}, bf16[1536,2048]{1,0:T(8,128)(2,1)})) %all-reduce.6.cloned.1.call-update) | async-done | bytes 12582928 | tf_op jit(solution)/shard_map/psum | solution.py:9
  348.6 0.0 slice-start.1
  348.6 0.0 slice-start.2
  348.6 16.3 %fusion.1 = f32[2048,1536]{1,0:T(8,128)} fusion(bf16[1536,2048]{1,0:T(8,128)(2,1)} %get-tuple-element.2, bf16[1536,3072]{1,0:T(8,128)(2,1)} %param.4), kind=kOutput, calls=%fused_computation.4 | convolution fusion | flops 9663676416 | bytes 23592960 | tf_op jit(solution)/shard_map/dot_general | solution.py:35
  364.8 0.0 slice-done
  364.9 0.0 slice-done.1
  364.9 0.0 slice-done.2
  364.9 16.9 %convolution_add_fusion = f32[2048,1536]{1,0:T(8,128)} fusion(f32[2048,1536]{1,0:T(8,128)} %fusion.1, bf16[1536,2048]{1,0:T(8,128)(2,1)} %get-tuple-element.3, bf16[1536,3072]{1,0:T(8,128)(2,1)S(1)} %bitcast.15), kind=kOutput, calls=%fused_computation | convolution fusion | flops 9666822144 | bytes 36175872 | tf_op jit(solution)/shard_map/dot_general | solution.py:35
  381.8 0.0 copy-start
  381.8 0.0 reduce-scatter.2.cloned.1.call-update
  381.8 0.2 all-reduce.4.cloned.1.call-start
  382.1 1.2 copy-done
  383.2 1.6 copy.8
  384.8 118.0 %reduce-scatter.2.cloned.1.call-done = f32[512,1536]{1,0:T(8,128)} async-done(((f32[2048,1536]{1,0:T(8,128)}), f32[512,1536]{1,0:T(8,128)}) %reduce-scatter.2.cloned.1.call-update) | async-done | bytes 3145744 | tf_op jit(solution)/shard_map/reduce_scatter | solution.py:38
  502.7 0.0 copy-start.1
  502.7 4.8 convolution_convert_fusion
  507.6 0.0 all-reduce.4.cloned.1.call-update
  507.6 0.0 copy-done.1
  507.6 1.5 negate_convert_fusion
  509.1 53.6 %all-reduce.4.cloned.1.call-done = bf16[4,128,128]{2,1,0:T(8,128)(2,1)} async-done(((bf16[4,128,128]{2,1,0:T(8,128)(2,1)}), bf16[4,128,128]{2,1,0:T(8,128)(2,1)}) %all-reduce.4.cloned.1.call-update) | async-done | bytes 131088 | tf_op jit(solution)/shard_map/psum | solution.py:44
  562.7 1.7 convert_add_fusion
  (1 shorter events, 0.0 us)
Async XLA Ops:
  7.2 78.5 %all-gather.2.cloned.1.call-start = ((), (), s32[]{:S(2)}) async-start(), calls=%async_computation.1 | async-start | bytes 7864320 | tf_op jit(solution)/shard_map/all_gather | solution.py:26
  12.9 335.7 %all-reduce.6.cloned.1.call-start = ((), (), s32[]{:S(2)}) async-start(), calls=%async_computation.4 | async-start | bytes 25165824 | tf_op jit(solution)/shard_map/psum | solution.py:9
  93.8 271.1 %slice-start = ((s8[9437184]{0:T(1024)(128)(4,1)}), s8[1048576]{0:T(1024)(128)(4,1)S(1)}, s32[]{:S(2)}) async-start(s8[9437184]{0:T(1024)(128)(4,1)} %bitcast.14), calls=%async_computation.5 | async-start | bytes 2097152
  93.8 408.9 %reduce-scatter.2.cloned.1.call-start = ((), (), s32[]{:S(2)}) async-start(), calls=%async_computation.2 | async-start | bytes 15728640 | tf_op jit(solution)/shard_map/reduce_scatter | solution.py:38
  348.6 16.3 %slice-start.1 = ((s8[9437184]{0:T(1024)(128)(4,1)}), s8[4194304]{0:T(1024)(128)(4,1)S(1)}, s32[]{:S(2)}) async-start(s8[9437184]{0:T(1024)(128)(4,1)} %bitcast.14), calls=%async_computation.6 | async-start | bytes 8388608
  348.6 16.3 %slice-start.2 = ((s8[9437184]{0:T(1024)(128)(4,1)}), s8[4194304]{0:T(1024)(128)(4,1)S(1)}, s32[]{:S(2)}) async-start(s8[9437184]{0:T(1024)(128)(4,1)} %bitcast.14), calls=%async_computation.7 | async-start | bytes 8388608
  381.8 1.4 copy-start
  381.8 180.9 %all-reduce.4.cloned.1.call-start = ((), (), s32[]{:S(2)}) async-start(), calls=%async_computation.3 | async-start | bytes 262144 | tf_op jit(solution)/shard_map/psum | solution.py:44
  502.7 4.9 copy-start.1
Sparse Core Ops, SparseCore 0:
  13.0 72.6 all-gather.1
  93.9 254.5 all-reduce.5
  381.9 120.7 reduce-scatter.1
  507.7 54.9 all-reduce.3
where the time goes:
time: 571 us
  waiting for transfers between devices  499 us (87%)
  matrix products  38 us (7%)
  other arithmetic  14.9 us (3%)
  between operations  13.8 us (2%)
    psum x1, waiting for transfers between devices, from_root(): return lax.psum(kept, axis)  255 us
    reduce_scatter x1, waiting for transfers between devices, per_device(): reduced = lax.psum_scatter(summed, 'col', scatter_dimension=0, tiled=True)  118 us
    all_gather x1, waiting for transfers between devices, per_device(): full_rows = lax.all_gather(masked, 'col', axis=1, tiled=True)  72.7 us
    psum x1, waiting for transfers between devices, per_device(): lax.psum(partial_diag.astype(jnp.bfloat16), 'row').astype(jnp.float32)  53.6 us
    dot_general x2, matrix products, per_device(): lax.dot_general(columns, inverse_part, (((0,), (1,)), ((), ())), preferre...  33.2 us
  transfers between devices with their start and end apart: 4, of which 4 were waited for; matrix products, arithmetic and copies ran while one was open for 1% of the time, Pallas kernels for 0%

commit v1 on v0

--- a/solution.py
+++ b/solution.py
@@ -4,9 +4,15 @@
 from jax.sharding import PartitionSpec as P
 
 
+def summed_here(shard, name):
+    parts = lax.all_gather(shard, name, axis=0, tiled=False)
+    acc = parts.sum(axis=0)
+    return acc
+
+
 def from_root(value, axis, source):
     kept = jnp.where(lax.axis_index(axis) == source, value, 0).astype(value.dtype)
-    return lax.psum(kept, axis)
+    return summed_here(kept, axis)
 
 
 def per_device(inverse_tiles, factor, block_mask, diag_inverse):

time: 571 us -> 1190 us (2.08)
  waiting for transfers between devices: 499 us -> 1070 us
  other arithmetic: 14.9 us -> 62.9 us
    all_gather x0 -> x2, waiting for transfers between devices: none -> 826 us  [summed_here(): parts = lax.all_gather(shard, name, axis=0, tiled=False)]
    psum x1 -> x0, waiting for transfers between devices: 255 us -> none  [from_root(): return lax.psum(kept, axis)]
    reduce_sum x0 -> x2, other arithmetic: none -> 48.1 us  [summed_here(): acc = parts.sum(axis=0)]
  transfers between devices with their start and end apart: 4 -> 5, of which waited for: 4 -> 5; matrix products, arithmetic and copies ran while one was open for 1% -> 3% of each run, Pallas kernels for 0% -> 0%
where the time goes in v1:
time: 1190 us
  waiting for transfers between devices  1070 us (90%)
  other arithmetic  62.9 us (5%)
  matrix products  37.2 us (3%)
  between operations  13.8 us (1%)
    all_gather x2, waiting for transfers between devices, summed_here(): parts = lax.all_gather(shard, name, axis=0, tiled=False)  826 us
    reduce_scatter x1, waiting for transfers between devices, per_device(): reduced = lax.psum_scatter(summed, 'col', scatter_dimension=0, tiled=True)  116 us
    all_gather x1, waiting for transfers between devices, per_device(): full_rows = lax.all_gather(masked, 'col', axis=1, tiled=True)  72.7 us
    psum x1, waiting for transfers between devices, per_device(): lax.psum(partial_diag.astype(jnp.bfloat16), 'row').astype(jnp.float32)  53.6 us
    reduce_sum x2, other arithmetic, summed_here(): acc = parts.sum(axis=0)  48.1 us
    dot_general x2, matrix products, per_device(): lax.dot_general(columns, inverse_part, (((0,), (1,)), ((), ())), preferre...  32.4 us
  transfers between devices with their start and end apart: 5, of which 5 were waited for; matrix products, arithmetic and copies ran while one was open for 3% of the time, Pallas kernels for 0%

profile of v1, /device:TPU:0, one launch (start us, length us, event | category | flops | bytes accessed | tf_op | source)
XLA Modules:
  0.0 1188.2 jit_solution(15474356219883665549)
XLA Ops:
  7.2 0.0 all-gather.6.cloned.1.call-start
  7.2 0.8 dynamic-slice_convert_fusion
  8.0 0.1 copy.6
  8.1 0.1 broadcast_in_dim.11
  8.2 1.9 broadcast_in_dim.12
  10.1 2.8 bitcast_multiply_fusion
  12.9 0.0 all-gather.6.cloned.1.call-update
  12.9 0.0 all-gather.10.cloned.1.call-start
  12.9 72.7 %all-gather.6.cloned.1.call-done = bf16[1536,2048]{1,0:T(8,128)(2,1)} async-done(((bf16[1536,512]{1,0:T(8,128)(2,1)}), bf16[1536,2048]{1,0:T(8,128)(2,1)}) %all-gather.6.cloned.1.call-update) | async-done | bytes 6291472 | tf_op jit(solution)/shard_map/all_gather | solution.py:32
  85.7 8.1 broadcast_select_fusion
  93.7 0.0 all-gather.10.cloned.1.call-update
  93.8 0.0 all-gather.8.cloned.1.call-start
  93.8 0.7 all-gather.8.cloned.1.call-update
  94.5 0.0 reduce-scatter.2.cloned.1.call-start
  94.5 426.7 %all-gather.10.cloned.1.call-done = bf16[12288,2048]{1,0:T(8,128)(2,1)} async-done(((bf16[1536,2048]{1,0:T(8,128)(2,1)}), bf16[12288,2048]{1,0:T(8,128)(2,1)}) %all-gather.10.cloned.1.call-update) | async-done | bytes 50331664 | tf_op jit(solution)/shard_map/all_gather | solution.py:8
  521.3 28.1 %reduce_sum.25 = bf16[1536,2048]{1,0:T(8,128)(2,1)} reduce(bf16[8,1536,2048]{2,1,0:T(8,128)(2,1)} %bitcast.12, bf16[]{:T(256)} %constant.26.clone.1), dimensions={0}, to_apply=%region_1.2 | reduce | flops 22020096 | bytes 56623104 | tf_op jit(solution)/shard_map/reduce_sum | solution.py:9
  549.4 399.2 %all-gather.8.cloned.1.call-done = bf16[12288,2048]{1,0:T(8,128)(2,1)} async-done(((bf16[1536,2048]{1,0:T(8,128)(2,1)}), bf16[12288,2048]{1,0:T(8,128)(2,1)}) %all-gather.8.cloned.1.call-update) | async-done | bytes 50331664 | tf_op jit(solution)/shard_map/all_gather | solution.py:8
  948.5 0.0 slice-start
  948.5 20.0 %reduce_sum.24 = bf16[1536,2048]{1,0:T(8,128)(2,1)} reduce(bf16[8,1536,2048]{2,1,0:T(8,128)(2,1)} %bitcast.13, bf16[]{:T(256)} %constant.26.clone.1), dimensions={0}, to_apply=%region_0.1 | reduce | flops 22020096 | bytes 56623104 | tf_op jit(solution)/shard_map/reduce_sum | solution.py:9
  968.6 0.0 slice-start.1
  968.6 16.3 %fusion.1 = f32[2048,1536]{1,0:T(8,128)} fusion(bf16[1536,2048]{1,0:T(8,128)(2,1)} %reduce_sum.24, bf16[1536,3072]{1,0:T(8,128)(2,1)} %param.4), kind=kOutput, calls=%fused_computation.4 | convolution fusion | flops 9663676416 | bytes 23592960 | tf_op jit(solution)/shard_map/dot_general | solution.py:41
  984.9 0.0 slice-done
  984.9 0.0 slice-done.1
  984.9 16.1 %convolution_add_fusion = f32[2048,1536]{1,0:T(8,128)} fusion(f32[2048,1536]{1,0:T(8,128)} %fusion.1, bf16[1536,2048]{1,0:T(8,128)(2,1)S(1)} %bitcast.18, bf16[1536,3072]{1,0:T(8,128)(2,1)} %param.4), kind=kOutput, calls=%fused_computation | convolution fusion | flops 9666822144 | bytes 36175872 | tf_op jit(solution)/shard_map/dot_general | solution.py:41
  1001.0 0.0 copy-start
  1001.0 0.0 reduce-scatter.2.cloned.1.call-update
  1001.0 0.2 all-reduce.2.cloned.1.call-start
  1001.2 1.2 copy-done
  1002.4 1.6 copy.8
  1003.9 116.0 %reduce-scatter.2.cloned.1.call-done = f32[512,1536]{1,0:T(8,128)} async-done(((f32[2048,1536]{1,0:T(8,128)}), f32[512,1536]{1,0:T(8,128)}) %reduce-scatter.2.cloned.1.call-update) | async-done | bytes 3145744 | tf_op jit(solution)/shard_map/reduce_scatter | solution.py:44
  1119.9 0.0 copy-start.1
  1119.9 4.8 convolution_convert_fusion
  1124.8 0.0 all-reduce.2.cloned.1.call-update
  1124.8 0.0 copy-done.1
  1124.8 1.5 negate_convert_fusion
  1126.3 53.6 %all-reduce.2.cloned.1.call-done = bf16[4,128,128]{2,1,0:T(8,128)(2,1)} async-done(((bf16[4,128,128]{2,1,0:T(8,128)(2,1)}), bf16[4,128,128]{2,1,0:T(8,128)(2,1)}) %all-reduce.2.cloned.1.call-update) | async-done | bytes 131088 | tf_op jit(solution)/shard_map/psum | solution.py:50
  1179.9 1.7 convert_add_fusion
  (1 shorter events, 0.0 us)
Async XLA Ops:
  7.2 78.5 %all-gather.6.cloned.1.call-start = ((), (), s32[]{:S(2)}) async-start(), calls=%async_computation.1 | async-start | bytes 7864320 | tf_op jit(solution)/shard_map/all_gather | solution.py:32
  12.9 508.4 %all-gather.10.cloned.1.call-start = ((), (), s32[]{:S(2)}) async-start(), calls=%async_computation.5 | async-start | bytes 56623104 | tf_op jit(solution)/shard_map/all_gather | solution.py:8
  93.8 854.8 %all-gather.8.cloned.1.call-start = ((), (), s32[]{:S(2)}) async-start(), calls=%async_computation.4 | async-start | bytes 56623104 | tf_op jit(solution)/shard_map/all_gather | solution.py:8
  94.5 1025.4 %reduce-scatter.2.cloned.1.call-start = ((), (), s32[]{:S(2)}) async-start(), calls=%async_computation.2 | async-start | bytes 15728640 | tf_op jit(solution)/shard_map/reduce_scatter | solution.py:44
  948.5 36.3 %slice-start = ((s8[6291456]{0:T(1024)(128)(4,1)}), s8[2097152]{0:T(1024)(128)(4,1)S(1)}, s32[]{:S(2)}) async-start(s8[6291456]{0:T(1024)(128)(4,1)} %bitcast.17), calls=%async_computation.6 | async-start | bytes 4194304
  968.6 16.3 %slice-start.1 = ((s8[6291456]{0:T(1024)(128)(4,1)}), s8[4194304]{0:T(1024)(128)(4,1)S(1)}, s32[]{:S(2)}) async-start(s8[6291456]{0:T(1024)(128)(4,1)} %bitcast.17), calls=%async_computation.7 | async-start | bytes 8388608
  1001.0 1.4 copy-start
  1001.0 178.9 %all-reduce.2.cloned.1.call-start = ((), (), s32[]{:S(2)}) async-start(), calls=%async_computation.3 | async-start | bytes 262144 | tf_op jit(solution)/shard_map/psum | solution.py:50
  1119.9 4.9 copy-start.1
Sparse Core Ops, SparseCore 0:
  13.0 72.6 all-gather.5
  93.9 427.3 all-gather.9
  522.9 425.5 all-gather.7
  1001.1 118.7 reduce-scatter.1
  1124.9 54.9 all-reduce.1
